TPU v7x, 32 devices: a whole 2x2x4 slice. The times are simulated.
32 devices in a mesh: band: 8 (over z, y), dir: 4 (over x, core).
Axes of the slice: x: 2, y: 2, z: 4, core: 2. Of those that a mesh axis runs over, the one named last changes fastest.
Arguments:
- visibilities: float32 [8, 2, 2, 2, 16, 512], P('band'), may hold values from -6 to 6
- coherencies: float32 [8, 16, 2, 2, 2, 16, 512], P('band', 'dir'), may hold values from -1.2 to 1.2
- jones_start: float32 [8, 16, 2, 2, 2, 1024], P('band', 'dir'), may hold values from -3.6 to 3.6
- dual_start: float32 [8, 16, 2, 2, 2, 1024], P('band', 'dir'), may hold values from -6 to 6
- consensus_start: float32 [8, 16, 2, 2, 2, 1024], P(None, 'dir'), may hold values from -1.8 to 1.8
- freq_basis: float32 [8, 8], P('band'), may hold values from -1 to 1
- baseline_station_pairs: int32 [2, 512], replicated, may hold values from 0 to 1023
Outputs:
- jones_final: float32 [8, 16, 2, 2, 2, 1024], P('band', 'dir')
- dual_final: float32 [8, 16, 2, 2, 2, 1024], P('band', 'dir')
- consensus_coeffs: float32 [8, 16, 2, 2, 2, 1024], P(None, 'dir')
All inputs are finite; a program needn't handle non-finite values.
Results may differ from a plain program's by a relative error of at most 0.0003.
Values sent between devices are 32-bit elements; how exact they have to be, the bound alone decides.
No kernel may reach another device: no remote copies, remote signals or barrier semaphores. Data moves between devices by JAX's collectives and lax.ppermute only.
A program may use at most 128 MiB of HBM per device.

v0:
```python
import jax
import jax.numpy as jnp
from jax import lax
from jax.sharding import PartitionSpec as P

ITERS = 3
RHO = 5.0
RIDGE = 0.25


def small_mul(left, right):
    return left[:, 0:1] * right[0:1] + left[:, 1:2] * right[1:2]


def complex_mul(left, right):
    real_part = small_mul(left[0], right[0]) - small_mul(left[1], right[1])
    imag_part = small_mul(left[0], right[1]) + small_mul(left[1], right[0])
    return jnp.stack([real_part, imag_part])


def hermitian(value):
    return jnp.stack([jnp.swapaxes(value[0], 0, 1), -jnp.swapaxes(value[1], 0, 1)])


def solve_right(numer, matrix):
    adjugate = jnp.stack(
        [
            jnp.stack([matrix[:, 1, 1], -matrix[:, 0, 1]], axis=1),
            jnp.stack([-matrix[:, 1, 0], matrix[:, 0, 0]], axis=1),
        ],
        axis=1,
    )
    det_real = (
        matrix[0, 0, 0] * matrix[0, 1, 1]
        - matrix[1, 0, 0] * matrix[1, 1, 1]
        - (matrix[0, 0, 1] * matrix[0, 1, 0] - matrix[1, 0, 1] * matrix[1, 1, 0])
    )
    det_imag = (
        matrix[0, 0, 0] * matrix[1, 1, 1]
        + matrix[1, 0, 0] * matrix[0, 1, 1]
        - (matrix[0, 0, 1] * matrix[1, 1, 0] + matrix[1, 0, 1] * matrix[0, 1, 0])
    )
    product = complex_mul(numer, adjugate)
    divisor = det_real * det_real + det_imag * det_imag
    real_part = (product[0] * det_real + product[1] * det_imag) / divisor
    imag_part = (product[1] * det_real - product[0] * det_imag) / divisor
    return jnp.stack([real_part, imag_part])


def predict(jones_k, coher_k, first, second):
    jones_first = jnp.take(jones_k, first, axis=-1)[..., None, :]
    jones_second = jnp.take(jones_k, second, axis=-1)[..., None, :]
    return complex_mul(complex_mul(jones_first, coher_k), hermitian(jones_second))


def baseline_terms(target, jones_k, coher_k, first, second):
    jones_first = jnp.take(jones_k, first, axis=-1)[..., None, :]
    jones_second = jnp.take(jones_k, second, axis=-1)[..., None, :]
    along_term = complex_mul(coher_k, hermitian(jones_second))
    back_term = hermitian(complex_mul(jones_first, coher_k))
    flipped = hermitian(target)
    right_first = jnp.sum(complex_mul(target, hermitian(along_term)), axis=-2)
    normal_first = jnp.sum(complex_mul(along_term, hermitian(along_term)), axis=-2)
    right_second = jnp.sum(complex_mul(flipped, hermitian(back_term)), axis=-2)
    normal_second = jnp.sum(complex_mul(back_term, hermitian(back_term)), axis=-2)
    first_part = jnp.concatenate([right_first.reshape(8, -1), normal_first.reshape(8, -1)], axis=0)
    second_part = jnp.concatenate(
        [right_second.reshape(8, -1), normal_second.reshape(8, -1)], axis=0
    )
    return jnp.concatenate([first_part, second_part], axis=1)


def update_one(right_sum, normal_sum, consensus, dual):
    identity = jnp.stack([jnp.eye(2, dtype=jnp.float32), jnp.zeros((2, 2), jnp.float32)])[..., None]
    matrix = normal_sum + RHO * identity
    return solve_right(right_sum + RHO * consensus - dual, matrix)


def apply_inverse(scale_factor, sums):
    flat = sums.reshape(sums.shape[0], -1)
    return jax.scipy.linalg.cho_solve((scale_factor, True), flat).reshape(sums.shape)


def local(
    visibilities,
    coherencies,
    jones_start,
    dual_start,
    consensus_start,
    freq_basis,
    baseline_station_pairs,
):
    coefficient_row = freq_basis[0]
    terms = coefficient_row.shape[0]
    outer = coefficient_row[:, None] * coefficient_row[None, :]
    gram = lax.psum(outer, "band") + RIDGE * lax.axis_size("band") * jnp.eye(
        terms, dtype=jnp.float32
    )
    scale_factor = jnp.linalg.cholesky(gram)
    first = baseline_station_pairs[0]
    second = baseline_station_pairs[1]
    stations = jones_start.shape[-1]
    station_ids = jnp.arange(stations, dtype=jnp.int32)
    onehots = (jnp.concatenate([first, second])[:, None] == station_ids[None, :]).astype(
        jnp.float32
    )
    vis_band = visibilities[0]
    coher_band = coherencies[0]
    jones = jones_start[0]
    dual = dual_start[0]
    dirs = jones.shape[0]
    coeffs = consensus_start
    consensus = jnp.tensordot(coefficient_row, coeffs, axes=(0, 0), precision=lax.Precision.HIGHEST)
    for turn_index in range(ITERS):
        model_terms = jax.vmap(predict, (0, 0, None, None))(jones, coher_band, first, second)
        model_total = lax.psum(jnp.sum(model_terms, axis=0), "dir")
        residual = vis_band - model_total
        normal_terms = jax.vmap(baseline_terms, (0, 0, 0, None, None))(
            residual[None] + model_terms, jones, coher_band, first, second
        )
        stacked = normal_terms.reshape(dirs * 16, -1)
        segment = jnp.dot(stacked, onehots, precision=lax.Precision.HIGHEST)
        segment = segment.reshape((dirs, 2, 2, 2, 2, stations))
        jones = jax.vmap(update_one)(segment[:, 0], segment[:, 1], consensus, dual)
        local_terms = coefficient_row.reshape((terms, 1, 1, 1, 1, 1)) * (jones + dual / RHO)[None]
        coeff_sums = lax.psum(local_terms, "band")
        coeffs = apply_inverse(scale_factor, coeff_sums)
        consensus = jnp.tensordot(
            coefficient_row, coeffs, axes=(0, 0), precision=lax.Precision.HIGHEST
        )
        dual = dual + RHO * (jones - consensus)
    return (jones[None], dual[None], coeffs)


def solution(mesh):
    in_specs = (
        P("band", None, None, None, None, None),
        P("band", "dir", None, None, None, None, None),
        P("band", "dir", None, None, None, None),
        P("band", "dir", None, None, None, None),
        P(None, "dir", None, None, None, None),
        P("band", None),
        P(),
    )
    out_specs = (
        P("band", "dir", None, None, None, None),
        P("band", "dir", None, None, None, None),
        P(None, "dir", None, None, None, None),
    )
    return jax.shard_map(local, mesh=mesh, in_specs=in_specs, out_specs=out_specs, check_vma=False)
```

profile of v0, /device:TPU:0, one launch (start us, length us, event | category | flops | bytes accessed | tf_op | source)
XLA Modules:
  0.0 537.6 jit_solution(1846712404722757130)
XLA Ops:
  8.1 2.3 slice_bitcast_fusion.13
  10.4 4.4 copy.255
  14.8 7.1 %gather_fusion = f32[512,4,2,2,2]{1,4,3,2,0:T(2,128)} fusion(f32[4,2,2,2,1024]{0,3,4,2,1:T(2,128)} %bitcast.712, s32[1024]{0:T(1024)S(1)} %pad_clamp_fusion.1), kind=kCustom, calls=%fused_computation.clone | custom fusion | bytes 133120 | tf_op jit(solution)/shard_map/vmap(jit(_take))/gather | solution.py:51
  22.0 3.1 select_bitcast_fusion.5
  28.2 7.2 %gather_fusion.1 = f32[512,4,2,2,2]{1,4,3,2,0:T(2,128)} fusion(f32[4,2,2,2,1024]{0,3,4,2,1:T(2,128)} %bitcast.713, s32[1024]{0:T(1024)S(1)} %pad_clamp_fusion), kind=kCustom, calls=%fused_computation.1.clone | custom fusion | bytes 133120 | tf_op jit(solution)/shard_map/vmap(jit(_take))/gather | solution.py:52
  35.4 3.4 select_bitcast_fusion.4
  39.6 2.6 fusion.90
  62.5 2.1 fusion.13
  64.8 23.1 %psum.51 = f32[8,8]{0,1:T(8,128)S(1)} all-reduce(f32[8,8]{0,1:T(8,128)S(1)} %broadcast_multiply_fusion.3), channel_id=1, replica_groups=mesh['band'=8,'dir'=4] {'band'}, use_global_device_ids=true, to_apply=%region_12.14 | all-reduce | flops 64 | bytes 512 | tf_op jit(solution)/shard_map/psum | solution.py:96
  101.2 4.6 copy.288
  105.8 7.1 %gather_fusion.2 = f32[512,4,2,2,2]{1,4,3,2,0:T(2,128)} fusion(f32[4,2,2,2,1024]{0,3,4,2,1:T(2,128)} %copy.288, s32[1024]{0:T(1024)S(1)} %pad_clamp_fusion.1), kind=kCustom, calls=%fused_computation.2.clone | custom fusion | bytes 133120 | tf_op jit(solution)/shard_map/vmap(jit(_take))/gather | solution.py:51
  112.9 7.1 %gather_fusion.3 = f32[512,4,2,2,2]{1,4,3,2,0:T(2,128)} fusion(f32[4,2,2,2,1024]{0,3,4,2,1:T(2,128)} %copy.288, s32[1024]{0:T(1024)S(1)} %copy-done.112), kind=kCustom, calls=%fused_computation.3.clone | custom fusion | bytes 133120 | tf_op jit(solution)/shard_map/vmap(jit(_take))/gather | solution.py:52
  120.1 3.0 select_bitcast_fusion.3
  140.5 2.0 select_bitcast_fusion.2
  148.4 2.5 fusion.86
  153.6 2.1 add_subtract_fusion.15
  159.1 2.0 slice_bitcast_fusion.49
  168.2 1.9 slice_bitcast_fusion.63
  170.6 18.1 %all-reduce.10.cloned.1.call-done = f32[2,2,2,16,512]{4,3,2,1,0:T(8,128)} async-done(((f32[2,2,2,16,512]{4,3,2,1,0:T(8,128)}), f32[2,2,2,16,512]{4,3,2,1,0:T(8,128)}) %all-reduce.10.cloned.1.call-update) | async-done | bytes 262160 | tf_op jit(solution)/shard_map/psum | solution.py:116
  196.1 2.4 fusion.3
  198.6 72.6 %all-reduce.12.cloned.1.call-done = f32[8,32768]{1,0:T(8,128)} async-done(((f32[8,32768]{1,0:T(8,128)}), f32[8,32768]{1,0:T(8,128)}) %all-reduce.12.cloned.1.call-update) | async-done | bytes 1048592 | tf_op jit(solution)/shard_map/psum | solution.py:126
  271.1 2.3 fusion.68
  276.8 4.6 copy.327
  281.4 7.1 %gather_fusion.4 = f32[512,4,2,2,2]{1,4,3,2,0:T(2,128)} fusion(f32[4,2,2,2,1024]{0,3,4,2,1:T(2,128)} %copy.327, s32[1024]{0:T(1024)S(1)} %pad_clamp_fusion.1), kind=kCustom, calls=%fused_computation.4.clone | custom fusion | bytes 133120 | tf_op jit(solution)/shard_map/vmap(jit(_take))/gather | solution.py:51
  288.5 7.1 %gather_fusion.5 = f32[512,4,2,2,2]{1,4,3,2,0:T(2,128)} fusion(f32[4,2,2,2,1024]{0,3,4,2,1:T(2,128)} %copy.327, s32[1024]{0:T(1024)S(1)} %copy-done.113), kind=kCustom, calls=%fused_computation.5.clone | custom fusion | bytes 133120 | tf_op jit(solution)/shard_map/vmap(jit(_take))/gather | solution.py:52
  295.6 3.0 select_bitcast_fusion.1
  312.9 2.0 select_bitcast_fusion
  332.9 22.8 %all-reduce.14.cloned.1.call-done = f32[2,2,2,16,512]{4,3,2,1,0:T(8,128)} async-done(((f32[2,2,2,16,512]{4,3,2,1,0:T(8,128)}), f32[2,2,2,16,512]{4,3,2,1,0:T(8,128)}) %all-reduce.14.cloned.1.call-update) | async-done | bytes 262160 | tf_op jit(solution)/shard_map/psum | solution.py:116
  363.6 74.3 %all-reduce.16.cloned.1.call-done = f32[8,32768]{1,0:T(8,128)} async-done(((f32[8,32768]{1,0:T(8,128)}), f32[8,32768]{1,0:T(8,128)}) %all-reduce.16.cloned.1.call-update) | async-done | bytes 1048592 | tf_op jit(solution)/shard_map/psum | solution.py:126
  437.9 2.3 fusion.64
  446.2 77.2 %all-reduce.18.cloned.1.call-done = f32[8,32768]{1,0:T(8,128)} async-done(((f32[8,32768]{1,0:T(8,128)}), f32[8,32768]{1,0:T(8,128)}) %all-reduce.18.cloned.1.call-update) | async-done | bytes 1048592 | tf_op jit(solution)/shard_map/psum | solution.py:126
  523.4 2.3 fusion.60
  (500 shorter events, 135.3 us)
Async XLA Ops:
  7.2 55.4 %copy-start = (f32[8,4,2,2,2,1024]{5,4,3,2,1,0:T(2,128)S(1)}, f32[8,4,2,2,2,1024]{5,4,3,2,1,0:T(2,128)}, u32[]{:S(2)}) copy-start(f32[8,4,2,2,2,1024]{5,4,3,2,1,0:T(2,128)} %param.15) | copy-start | bytes 3145732
  7.2 84.3 %all-reduce.8.cloned.1.call-start = ((), (), s32[]{:S(2)}) async-start(), calls=%async_computation | async-start | bytes 524288 | tf_op jit(solution)/shard_map/psum | solution.py:116
  8.1 13.9 %copy-start.117 = (pred[512]{0:T(512)(128)(4,1)}, pred[512]{0:T(512)(128)(4,1)S(1)}, u32[]{:S(2)}) copy-start(pred[512]{0:T(512)(128)(4,1)S(1)} %compare_and_fusion) | copy-start | bytes 1540
  8.1 27.3 %copy-start.114 = (pred[512]{0:T(512)(128)(4,1)}, pred[512]{0:T(512)(128)(4,1)S(1)}, u32[]{:S(2)}) copy-start(pred[512]{0:T(512)(128)(4,1)S(1)} %compare_and_fusion.1) | copy-start | bytes 1540
  28.2 10.5 %copy-start.111 = (s32[1024]{0:T(1024)}, s32[1024]{0:T(1024)S(1)}, u32[]{:S(2)}) copy-start(s32[1024]{0:T(1024)S(1)} %pad_clamp_fusion) | copy-start | bytes 12292
  48.1 140.6 %all-reduce.10.cloned.1.call-start = ((), (), s32[]{:S(2)}) async-start(), calls=%async_computation.1 | async-start | bytes 524288 | tf_op jit(solution)/shard_map/psum | solution.py:116
  60.0 31.6 %copy-start.12 = (f32[1,2,2,2,16,512]{5,4,3,2,1,0:T(8,128)S(1)}, f32[1,2,2,2,16,512]{5,4,3,2,1,0:T(8,128)}, u32[]{:S(2)}) copy-start(f32[1,2,2,2,16,512]{5,4,3,2,1,0:T(8,128)} %param.11) | copy-start | bytes 786436
  101.1 4.7 copy-start.89
  101.2 4.7 copy-start.92
  101.2 11.7 %copy-start.112 = (s32[1024]{0:T(1024)S(1)}, s32[1024]{0:T(1024)}, u32[]{:S(2)}) copy-start(s32[1024]{0:T(1024)} %copy-done.111) | copy-start | bytes 12292
  101.2 18.9 %copy-start.118 = (pred[512]{0:T(512)(128)(4,1)S(1)}, pred[512]{0:T(512)(128)(4,1)}, u32[]{:S(2)}) copy-start(pred[512]{0:T(512)(128)(4,1)} %copy-done.117) | copy-start | bytes 1540
  153.5 4.2 copy-start.79
  153.5 4.2 copy-start.80
  158.1 5.8 %copy-start.4 = (f32[1,4,2,2,16,512]{5,4,3,2,1,0:T(8,128)}, f32[1,4,2,2,16,512]{5,4,3,2,1,0:T(8,128)S(1)}, u32[]{:S(2)}) copy-start(f32[1,4,2,2,16,512]{5,4,3,2,1,0:T(8,128)S(1)} %get-tuple-element.80) | copy-start | bytes 1572868
  158.1 5.8 %copy-start.5 = (f32[1,4,2,2,16,512]{5,4,3,2,1,0:T(8,128)}, f32[1,4,2,2,16,512]{5,4,3,2,1,0:T(8,128)S(1)}, u32[]{:S(2)}) copy-start(f32[1,4,2,2,16,512]{5,4,3,2,1,0:T(8,128)S(1)} %get-tuple-element.81) | copy-start | bytes 1572868
  159.0 112.1 %all-reduce.12.cloned.1.call-start = ((), (), s32[]{:S(2)}) async-start(), calls=%async_computation.2 | async-start | bytes 2097152 | tf_op jit(solution)/shard_map/psum | solution.py:126
  159.1 4.8 copy-start.21
  159.1 5.6 %copy-start.19 = (f32[4,2,2,16,512]{4,3,1,0,2:T(8,128)S(1)}, f32[4,2,2,16,512]{4,3,1,0,2:T(8,128)}, u32[]{:S(2)}) copy-start(f32[4,2,2,16,512]{4,3,1,0,2:T(8,128)} %get-tuple-element.79) | copy-start | bytes 1572868
  161.1 4.5 copy-start.95
  170.1 185.6 %all-reduce.14.cloned.1.call-start = ((), (), s32[]{:S(2)}) async-start(), calls=%async_computation.3 | async-start | bytes 524288 | tf_op jit(solution)/shard_map/psum | solution.py:116
  276.7 4.7 copy-start.83
  276.7 4.7 copy-start.86
  276.7 11.7 %copy-start.113 = (s32[1024]{0:T(1024)S(1)}, s32[1024]{0:T(1024)}, u32[]{:S(2)}) copy-start(s32[1024]{0:T(1024)} %copy-done.111) | copy-start | bytes 12292
  276.8 18.9 %copy-start.119 = (pred[512]{0:T(512)(128)(4,1)S(1)}, pred[512]{0:T(512)(128)(4,1)}, u32[]{:S(2)}) copy-start(pred[512]{0:T(512)(128)(4,1)} %copy-done.117) | copy-start | bytes 1540
  322.8 4.5 copy-start.20
  323.6 114.3 %all-reduce.16.cloned.1.call-start = ((), (), s32[]{:S(2)}) async-start(), calls=%async_computation.4 | async-start | bytes 2097152 | tf_op jit(solution)/shard_map/psum | solution.py:126
  323.7 4.5 copy-start.18
  324.6 4.5 copy-start.26
  324.6 4.5 copy-start.84
  324.6 4.5 copy-start.87
  332.6 190.8 %all-reduce.18.cloned.1.call-start = ((), (), s32[]{:S(2)}) async-start(), calls=%async_computation.5 | async-start | bytes 2097152 | tf_op jit(solution)/shard_map/psum | solution.py:126
  525.7 4.7 copy-start.1
  (97 other events, 188.2 us)
Sparse Core Ops, SparseCore 0:
  48.3 34.9 all-reduce.7
  159.1 29.5 all-reduce.9
  192.8 78.2 all-reduce.11
  323.8 31.8 all-reduce.13
  359.6 78.2 all-reduce.15
  445.6 77.8 all-reduce.17
where the time goes:
time: 548 us; the launch traced here: 538 us
  waiting for transfers between devices  265 us (48%)
  local copies, waits for them, and re-layouts  155 us (28%)
  other arithmetic  56.7 us (10%)
  blocking collectives  23.1 us (4%)
  matrix products  20.7 us (4%)
  between operations  16.6 us (3%)
    psum x3, waiting for transfers between devices, local(): coeff_sums = lax.psum(local_terms, 'band')  224 us
    mul x92, local copies, waits for them, and re-layouts, small_mul(): return left[:, 0:1] * right[0:1] + left[:, 1:2] * right[1:2]  57.9 us
    psum x3, waiting for transfers between devices, local(): model_total = lax.psum(jnp.sum(model_terms, axis=0), 'dir')  40.9 us
    psum x1, blocking collectives, local(): lax.psum(outer, 'band')  23.1 us
    gather x3, local copies, waits for them, and re-layouts, predict(): jones_second = jnp.take(jones_k, second, axis=-1)[..., None, :]  21.4 us
    gather x3, local copies, waits for them, and re-layouts, predict(): jones_first = jnp.take(jones_k, first, axis=-1)[..., None, :]  21.3 us
    slice x10, local copies, waits for them, and re-layouts, small_mul(): return left[:, 0:1] * right[0:1] + left[:, 1:2] * right[1:2]  16.4 us
    unnamed x250, local copies, waits for them, and re-layouts  15.9 us
  transfers between devices with their start and end apart: 6, of which 5 were waited for; matrix products, arithmetic and copies ran while one was open for 10% of the time, Pallas kernels for 0%

commit v1 on v0

--- a/solution.py
+++ b/solution.py
@@ -6,6 +6,15 @@
 ITERS = 3
 RHO = 5.0
 RIDGE = 0.25
+
+
+def added_up(x, name):
+    size = lax.axis_size(name)
+    total, far = (x, 1)
+    while far < size:
+        total = total + lax.ppermute(total, name, [(i, i ^ far) for i in range(size)])
+        far = 2 * far
+    return total
 
 
 def small_mul(left, right):
@@ -123,7 +132,7 @@
         segment = segment.reshape((dirs, 2, 2, 2, 2, stations))
         jones = jax.vmap(update_one)(segment[:, 0], segment[:, 1], consensus, dual)
         local_terms = coefficient_row.reshape((terms, 1, 1, 1, 1, 1)) * (jones + dual / RHO)[None]
-        coeff_sums = lax.psum(local_terms, "band")
+        coeff_sums = added_up(local_terms, "band")
         coeffs = apply_inverse(scale_factor, coeff_sums)
         consensus = jnp.tensordot(
             coefficient_row, coeffs, axes=(0, 0), precision=lax.Precision.HIGHEST

time: 548 us -> 564 us (1.029)
  starting transfers between devices: 0.9 us -> 17.3 us
  other arithmetic: 56.7 us -> 69.1 us
  waiting for transfers between devices: 265 us -> 255 us
    psum x3 -> x0, waiting for transfers between devices: 224 us -> none  [local(): coeff_sums = lax.psum(local_terms, 'band')]
    ppermute x0 -> x9, waiting for transfers between devices: none -> 210 us  [added_up(): lax.ppermute(total, name, [(i, i ^ far) for i in range(size)])]
    ppermute x0 -> x9, starting transfers between devices: none -> 17.2 us  [added_up(): lax.ppermute(total, name, [(i, i ^ far) for i in range(size)])]
    add x0 -> x9, other arithmetic: none -> 11.2 us  [added_up(): total + lax.ppermute(total, name, [(i, i ^ far) for i in range(size)])]
    mul x92, local copies, waits for them, and re-layouts: 57.9 us -> 64.6 us  [small_mul(): return left[:, 0:1] * right[0:1] + left[:, 1:2] * right[1:2]]
    unnamed x250 -> x274, local copies, waits for them, and re-layouts: 15.9 us -> 11.9 us
  transfers between devices with their start and end apart: 6 -> 12, of which waited for: 5 -> 9; matrix products, arithmetic and copies ran while one was open for 10% -> 9% of each run, Pallas kernels for 0% -> 0%
where the time goes in v1:
time: 564 us; the launch traced here: 554 us
  waiting for transfers between devices  255 us (45%)
  local copies, waits for them, and re-layouts  155 us (27%)
  other arithmetic  69.1 us (12%)
  blocking collectives  23.1 us (4%)
  matrix products  17.5 us (3%)
  starting transfers between devices  17.3 us (3%)
  between operations  16.7 us (3%)
    ppermute x9, waiting for transfers between devices, added_up(): lax.ppermute(total, name, [(i, i ^ far) for i in range(size)])  210 us
    mul x92, local copies, waits for them, and re-layouts, small_mul(): return left[:, 0:1] * right[0:1] + left[:, 1:2] * right[1:2]  64.6 us
    psum x3, waiting for transfers between devices, local(): model_total = lax.psum(jnp.sum(model_terms, axis=0), 'dir')  44.8 us
    psum x1, blocking collectives, local(): lax.psum(outer, 'band')  23.1 us
    gather x3, local copies, waits for them, and re-layouts, predict(): jones_second = jnp.take(jones_k, second, axis=-1)[..., None, :]  21.5 us
    gather x3, local copies, waits for them, and re-layouts, predict(): jones_first = jnp.take(jones_k, first, axis=-1)[..., None, :]  21.4 us
    ppermute x9, starting transfers between devices, added_up(): lax.ppermute(total, name, [(i, i ^ far) for i in range(size)])  17.2 us
    slice x10, local copies, waits for them, and re-layouts, small_mul(): return left[:, 0:1] * right[0:1] + left[:, 1:2] * right[1:2]  17.1 us
  transfers between devices with their start and end apart: 12, of which 9 were waited for; matrix products, arithmetic and copies ran while one was open for 9% of the time, Pallas kernels for 0%

profile of v1, /device:TPU:0, one launch (start us, length us, event | category | flops | bytes accessed | tf_op | source)
XLA Modules:
  0.0 554.1 jit_solution(7045922903503104838)
XLA Ops:
  9.4 4.5 copy.255
  13.9 7.2 %gather_fusion = f32[512,4,2,2,2]{1,4,3,2,0:T(2,128)} fusion(f32[4,2,2,2,1024]{0,3,4,2,1:T(2,128)} %bitcast.712, s32[1024]{0:T(1024)S(1)} %pad_clamp_fusion.1), kind=kCustom, calls=%fused_computation.clone | custom fusion | bytes 133120 | tf_op jit(solution)/shard_map/vmap(jit(_take))/gather | solution.py:60
  21.1 3.1 select_bitcast_fusion.5
  24.9 2.6 fusion.95
  30.4 7.2 %gather_fusion.1 = f32[512,4,2,2,2]{1,4,3,2,0:T(2,128)} fusion(f32[4,2,2,2,1024]{0,3,4,2,1:T(2,128)} %bitcast.713, s32[1024]{0:T(1024)S(1)} %pad_clamp_fusion), kind=kCustom, calls=%fused_computation.1.clone | custom fusion | bytes 133120 | tf_op jit(solution)/shard_map/vmap(jit(_take))/gather | solution.py:61
  37.5 3.2 select_bitcast_fusion.4
  41.7 2.6 fusion.93
  64.4 2.1 fusion.13
  66.6 23.1 %psum.30 = f32[8,8]{0,1:T(8,128)S(1)} all-reduce(f32[8,8]{0,1:T(8,128)S(1)} %broadcast_multiply_fusion.3), channel_id=1, replica_groups=mesh['band'=8,'dir'=4] {'band'}, use_global_device_ids=true, to_apply=%region_12.14 | all-reduce | flops 64 | bytes 512 | tf_op jit(solution)/shard_map/psum | solution.py:105
  103.1 4.9 copy.288
  107.9 7.1 %gather_fusion.2 = f32[512,4,2,2,2]{1,4,3,2,0:T(2,128)} fusion(f32[4,2,2,2,1024]{0,3,4,2,1:T(2,128)} %copy.288, s32[1024]{0:T(1024)S(1)} %pad_clamp_fusion.1), kind=kCustom, calls=%fused_computation.2.clone | custom fusion | bytes 133120 | tf_op jit(solution)/shard_map/vmap(jit(_take))/gather | solution.py:60
  115.0 7.2 %gather_fusion.3 = f32[512,4,2,2,2]{1,4,3,2,0:T(2,128)} fusion(f32[4,2,2,2,1024]{0,3,4,2,1:T(2,128)} %copy.288, s32[1024]{0:T(1024)S(1)} %copy-done.124), kind=kCustom, calls=%fused_computation.3.clone | custom fusion | bytes 133120 | tf_op jit(solution)/shard_map/vmap(jit(_take))/gather | solution.py:61
  122.2 3.0 select_bitcast_fusion.3
  150.5 2.4 fusion.89
  170.1 20.6 %all-reduce.7.cloned.1.call-done = f32[2,2,2,16,512]{4,3,2,1,0:T(8,128)} async-done(((f32[2,2,2,16,512]{4,3,2,1,0:T(8,128)}), f32[2,2,2,16,512]{4,3,2,1,0:T(8,128)}) %all-reduce.7.cloned.1.call-update) | async-done | bytes 262160 | tf_op jit(solution)/shard_map/psum | solution.py:125
  197.8 21.1 %collective-permute-done.1 = f32[8,4,2,2,2,1024]{5,4,3,2,1,0:T(2,128)S(1)} collective-permute-done((f32[8,4,2,2,2,1024]{5,4,3,2,1,0:T(2,128)S(1)}, f32[8,4,2,2,2,1024]{5,4,3,2,1,0:T(2,128)S(1)}, u32[]{:S(2)}, u32[]{:S(2)}) %collective-permute-start.1) | collective-permute-done | bytes 1048608 | tf_op jit(solution)/shard_map/ppermute | solution.py:15
  218.9 2.2 fusion.112
  221.3 2.7 collective-permute-start.2
  226.0 2.4 fusion.3
  228.4 39.2 %collective-permute-done.2 = f32[8,4,2,2,2,1024]{5,4,3,2,1,0:T(2,128)S(1)} collective-permute-done((f32[8,4,2,2,2,1024]{5,4,3,2,1,0:T(2,128)S(1)}, f32[8,4,2,2,2,1024]{5,4,3,2,1,0:T(2,128)S(1)}, u32[]{:S(2)}, u32[]{:S(2)}) %collective-permute-start.2) | collective-permute-done | bytes 1048608 | tf_op jit(solution)/shard_map/ppermute | solution.py:15
  275.7 4.4 copy.327
  280.1 7.1 %gather_fusion.4 = f32[512,4,2,2,2]{1,4,3,2,0:T(2,128)} fusion(f32[4,2,2,2,1024]{0,3,4,2,1:T(2,128)} %copy.327, s32[1024]{0:T(1024)S(1)} %pad_clamp_fusion.1), kind=kCustom, calls=%fused_computation.4.clone | custom fusion | bytes 133120 | tf_op jit(solution)/shard_map/vmap(jit(_take))/gather | solution.py:60
  287.2 7.2 %gather_fusion.5 = f32[512,4,2,2,2]{1,4,3,2,0:T(2,128)} fusion(f32[4,2,2,2,1024]{0,3,4,2,1:T(2,128)} %copy.327, s32[1024]{0:T(1024)S(1)} %copy-done.125), kind=kCustom, calls=%fused_computation.5.clone | custom fusion | bytes 133120 | tf_op jit(solution)/shard_map/vmap(jit(_take))/gather | solution.py:61
  294.4 3.0 select_bitcast_fusion.1
  337.8 24.2 %all-reduce.9.cloned.1.call-done = f32[2,2,2,16,512]{4,3,2,1,0:T(8,128)} async-done(((f32[2,2,2,16,512]{4,3,2,1,0:T(8,128)}), f32[2,2,2,16,512]{4,3,2,1,0:T(8,128)}) %all-reduce.9.cloned.1.call-update) | async-done | bytes 262160 | tf_op jit(solution)/shard_map/psum | solution.py:125
  366.5 21.3 %collective-permute-done.4 = f32[8,4,2,2,2,1024]{5,4,3,2,1,0:T(2,128)S(1)} collective-permute-done((f32[8,4,2,2,2,1024]{5,4,3,2,1,0:T(2,128)S(1)}, f32[8,4,2,2,2,1024]{5,4,3,2,1,0:T(2,128)S(1)}, u32[]{:S(2)}, u32[]{:S(2)}) %collective-permute-start.4) | collective-permute-done | bytes 1048608 | tf_op jit(solution)/shard_map/ppermute | solution.py:15
  388.9 2.7 collective-permute-start.5
  395.4 40.0 %collective-permute-done.5 = f32[8,4,2,2,2,1024]{5,4,3,2,1,0:T(2,128)S(1)} collective-permute-done((f32[8,4,2,2,2,1024]{5,4,3,2,1,0:T(2,128)S(1)}, f32[8,4,2,2,2,1024]{5,4,3,2,1,0:T(2,128)S(1)}, u32[]{:S(2)}, u32[]{:S(2)}) %collective-permute-start.5) | collective-permute-done | bytes 1048608 | tf_op jit(solution)/shard_map/ppermute | solution.py:15
  443.5 22.4 %collective-permute-done.6 = f32[8,4,2,2,2,1024]{5,4,3,2,1,0:T(2,128)S(1)} collective-permute-done((f32[8,4,2,2,2,1024]{5,4,3,2,1,0:T(2,128)S(1)}, f32[8,4,2,2,2,1024]{5,4,3,2,1,0:T(2,128)S(1)}, u32[]{:S(2)}, u32[]{:S(2)}) %collective-permute-start.6) | collective-permute-done | bytes 1048608 | tf_op jit(solution)/shard_map/ppermute | solution.py:15
  468.4 22.5 %collective-permute-done.7 = f32[8,4,2,2,2,1024]{5,4,3,2,1,0:T(2,128)S(1)} collective-permute-done((f32[8,4,2,2,2,1024]{5,4,3,2,1,0:T(2,128)S(1)}, f32[8,4,2,2,2,1024]{5,4,3,2,1,0:T(2,128)S(1)}, u32[]{:S(2)}, u32[]{:S(2)}) %collective-permute-start.7) | collective-permute-done | bytes 1048608 | tf_op jit(solution)/shard_map/ppermute | solution.py:15
  491.9 3.5 collective-permute-start.8
  496.1 43.6 %collective-permute-done.8 = f32[8,4,2,2,2,1024]{5,4,3,2,1,0:T(2,128)S(1)} collective-permute-done((f32[8,4,2,2,2,1024]{5,4,3,2,1,0:T(2,128)S(1)}, f32[8,4,2,2,2,1024]{5,4,3,2,1,0:T(2,128)S(1)}, u32[]{:S(2)}, u32[]{:S(2)}) %collective-permute-start.8) | collective-permute-done | bytes 1048608 | tf_op jit(solution)/shard_map/ppermute | solution.py:15
  (542 shorter events, 167.0 us)
Async XLA Ops:
  7.2 57.2 %copy-start = (f32[8,4,2,2,2,1024]{5,4,3,2,1,0:T(2,128)S(1)}, f32[8,4,2,2,2,1024]{5,4,3,2,1,0:T(2,128)}, u32[]{:S(2)}) copy-start(f32[8,4,2,2,2,1024]{5,4,3,2,1,0:T(2,128)} %param.15) | copy-start | bytes 3145732
  7.2 86.2 %all-reduce.5.cloned.1.call-start = ((), (), s32[]{:S(2)}) async-start(), calls=%async_computation | async-start | bytes 524288 | tf_op jit(solution)/shard_map/psum | solution.py:125
  8.1 13.0 %copy-start.129 = (pred[512]{0:T(512)(128)(4,1)}, pred[512]{0:T(512)(128)(4,1)S(1)}, u32[]{:S(2)}) copy-start(pred[512]{0:T(512)(128)(4,1)S(1)} %compare_and_fusion) | copy-start | bytes 1540
  8.1 29.4 %copy-start.126 = (pred[512]{0:T(512)(128)(4,1)}, pred[512]{0:T(512)(128)(4,1)S(1)}, u32[]{:S(2)}) copy-start(pred[512]{0:T(512)(128)(4,1)S(1)} %compare_and_fusion.1) | copy-start | bytes 1540
  9.4 38.1 %copy-start.6 = (f32[4,2,2,16,512]{4,3,2,1,0:T(8,128)}, f32[4,2,2,16,512]{4,3,2,1,0:T(8,128)S(1)}, u32[]{:S(2)}) copy-start(f32[4,2,2,16,512]{4,3,2,1,0:T(8,128)S(1)} %get-tuple-element.139) | copy-start | bytes 1572868
  9.4 38.1 %copy-start.7 = (f32[4,2,2,16,512]{4,3,2,1,0:T(8,128)}, f32[4,2,2,16,512]{4,3,2,1,0:T(8,128)S(1)}, u32[]{:S(2)}) copy-start(f32[4,2,2,16,512]{4,3,2,1,0:T(8,128)S(1)} %get-tuple-element.140) | copy-start | bytes 1572868
  30.3 10.4 %copy-start.123 = (s32[1024]{0:T(1024)}, s32[1024]{0:T(1024)S(1)}, u32[]{:S(2)}) copy-start(s32[1024]{0:T(1024)S(1)} %pad_clamp_fusion) | copy-start | bytes 12292
  50.1 140.6 %all-reduce.7.cloned.1.call-start = ((), (), s32[]{:S(2)}) async-start(), calls=%async_computation.1 | async-start | bytes 524288 | tf_op jit(solution)/shard_map/psum | solution.py:125
  61.9 31.5 %copy-start.11 = (f32[1,2,2,2,16,512]{5,4,3,2,1,0:T(8,128)S(1)}, f32[1,2,2,2,16,512]{5,4,3,2,1,0:T(8,128)}, u32[]{:S(2)}) copy-start(f32[1,2,2,2,16,512]{5,4,3,2,1,0:T(8,128)} %param.11) | copy-start | bytes 786436
  103.0 4.9 copy-start.91
  103.0 4.9 copy-start.94
  103.1 12.0 %copy-start.124 = (s32[1024]{0:T(1024)S(1)}, s32[1024]{0:T(1024)}, u32[]{:S(2)}) copy-start(s32[1024]{0:T(1024)} %copy-done.123) | copy-start | bytes 12292
  103.1 19.2 %copy-start.130 = (pred[512]{0:T(512)(128)(4,1)S(1)}, pred[512]{0:T(512)(128)(4,1)}, u32[]{:S(2)}) copy-start(pred[512]{0:T(512)(128)(4,1)} %copy-done.129) | copy-start | bytes 1540
  160.0 5.8 %copy-start.4 = (f32[1,4,2,2,16,512]{5,4,3,2,1,0:T(8,128)}, f32[1,4,2,2,16,512]{5,4,3,2,1,0:T(8,128)S(1)}, u32[]{:S(2)}) copy-start(f32[1,4,2,2,16,512]{5,4,3,2,1,0:T(8,128)S(1)} %get-tuple-element.80) | copy-start | bytes 1572868
  160.0 5.8 %copy-start.5 = (f32[1,4,2,2,16,512]{5,4,3,2,1,0:T(8,128)}, f32[1,4,2,2,16,512]{5,4,3,2,1,0:T(8,128)S(1)}, u32[]{:S(2)}) copy-start(f32[1,4,2,2,16,512]{5,4,3,2,1,0:T(8,128)S(1)} %get-tuple-element.81) | copy-start | bytes 1572868
  161.0 201.0 %all-reduce.9.cloned.1.call-start = ((), (), s32[]{:S(2)}) async-start(), calls=%async_computation.2 | async-start | bytes 524288 | tf_op jit(solution)/shard_map/psum | solution.py:125
  161.0 4.8 copy-start.21
  161.0 5.7 %copy-start.19 = (f32[4,2,2,16,512]{4,3,1,0,2:T(8,128)S(1)}, f32[4,2,2,16,512]{4,3,1,0,2:T(8,128)}, u32[]{:S(2)}) copy-start(f32[4,2,2,16,512]{4,3,1,0,2:T(8,128)} %get-tuple-element.79) | copy-start | bytes 1572868
  169.3 24.0 %collective-permute-start = (f32[8,4,2,2,2,1024]{5,4,3,2,1,0:T(2,128)}, f32[8,4,2,2,2,1024]{5,4,3,2,1,0:T(2,128)}, u32[]{:S(2)}, u32[]{:S(2)}) collective-permute-start(f32[8,4,2,2,2,1024]{5,4,3,2,1,0:T(2,128)} %broadcast_multiply_fusion.2), channel_id=1, source_target_pairs={{0,4},{4,0},{8,12},{12,8},{16,20},{20,16},{24,28},{28,24},{1,5},{5... | collective-permute-start | bytes 3145736 | tf_op jit(solution)/shard_map/ppermute | solution.py:15
  195.4 23.5 %collective-permute-start.1 = (f32[8,4,2,2,2,1024]{5,4,3,2,1,0:T(2,128)S(1)}, f32[8,4,2,2,2,1024]{5,4,3,2,1,0:T(2,128)S(1)}, u32[]{:S(2)}, u32[]{:S(2)}) collective-permute-start(f32[8,4,2,2,2,1024]{5,4,3,2,1,0:T(2,128)S(1)} %fusion.80), channel_id=1, source_target_pairs={{0,8},{4,12},{8,0},{12,4},{16,24},{20,28},{24,16},{28,20},{1,9},{5... | collective-permute-start | bytes 3145736 | tf_op jit(solution)/shard_map/ppermute | solution.py:15
  221.3 46.3 %collective-permute-start.2 = (f32[8,4,2,2,2,1024]{5,4,3,2,1,0:T(2,128)S(1)}, f32[8,4,2,2,2,1024]{5,4,3,2,1,0:T(2,128)S(1)}, u32[]{:S(2)}, u32[]{:S(2)}) collective-permute-start(f32[8,4,2,2,2,1024]{5,4,3,2,1,0:T(2,128)S(1)} %fusion.112), channel_id=1, source_target_pairs={{0,16},{4,20},{8,24},{12,28},{16,0},{20,4},{24,8},{28,12},{1,17},{... | collective-permute-start | bytes 3145736 | tf_op jit(solution)/shard_map/ppermute | solution.py:15
  275.2 58.2 %copy-start.27 = (f32[4,2,2,2,1024]{4,0,3,2,1:T(4,128)}, f32[4,2,2,2,1024]{4,0,3,2,1:T(4,128)S(1)}, u32[]{:S(2)}) copy-start(f32[4,2,2,2,1024]{4,0,3,2,1:T(4,128)S(1)} %get-tuple-element.23) | copy-start | bytes 393220
  275.7 11.5 %copy-start.125 = (s32[1024]{0:T(1024)S(1)}, s32[1024]{0:T(1024)}, u32[]{:S(2)}) copy-start(s32[1024]{0:T(1024)} %copy-done.123) | copy-start | bytes 12292
  275.7 18.7 %copy-start.131 = (pred[512]{0:T(512)(128)(4,1)S(1)}, pred[512]{0:T(512)(128)(4,1)}, u32[]{:S(2)}) copy-start(pred[512]{0:T(512)(128)(4,1)} %copy-done.129) | copy-start | bytes 1540
  331.8 5.1 copy-start.16
  335.2 28.1 %collective-permute-start.3 = (f32[8,4,2,2,2,1024]{5,4,3,2,1,0:T(2,128)}, f32[8,4,2,2,2,1024]{5,4,3,2,1,0:T(2,128)S(1)}, u32[]{:S(2)}, u32[]{:S(2)}) collective-permute-start(f32[8,4,2,2,2,1024]{5,4,3,2,1,0:T(2,128)} %broadcast_multiply_fusion.1), channel_id=1, source_target_pairs={{0,4},{4,0},{8,12},{12,8},{16,20},{20,16},{24,28},{28,24},{1,5},{5... | collective-permute-start | bytes 3145736 | tf_op jit(solution)/shard_map/ppermute | solution.py:15
  364.1 23.7 %collective-permute-start.4 = (f32[8,4,2,2,2,1024]{5,4,3,2,1,0:T(2,128)S(1)}, f32[8,4,2,2,2,1024]{5,4,3,2,1,0:T(2,128)S(1)}, u32[]{:S(2)}, u32[]{:S(2)}) collective-permute-start(f32[8,4,2,2,2,1024]{5,4,3,2,1,0:T(2,128)S(1)} %fusion.81), channel_id=1, source_target_pairs={{0,8},{4,12},{8,0},{12,4},{16,24},{20,28},{24,16},{28,20},{1,9},{5... | collective-permute-start | bytes 3145736 | tf_op jit(solution)/shard_map/ppermute | solution.py:15
  388.9 46.5 %collective-permute-start.5 = (f32[8,4,2,2,2,1024]{5,4,3,2,1,0:T(2,128)S(1)}, f32[8,4,2,2,2,1024]{5,4,3,2,1,0:T(2,128)S(1)}, u32[]{:S(2)}, u32[]{:S(2)}) collective-permute-start(f32[8,4,2,2,2,1024]{5,4,3,2,1,0:T(2,128)S(1)} %fusion.111), channel_id=1, source_target_pairs={{0,16},{4,20},{8,24},{12,28},{16,0},{20,4},{24,8},{28,12},{1,17},{... | collective-permute-start | bytes 3145736 | tf_op jit(solution)/shard_map/ppermute | solution.py:15
  441.7 24.2 %collective-permute-start.6 = (f32[8,4,2,2,2,1024]{5,4,3,2,1,0:T(2,128)S(1)}, f32[8,4,2,2,2,1024]{5,4,3,2,1,0:T(2,128)S(1)}, u32[]{:S(2)}, u32[]{:S(2)}) collective-permute-start(f32[8,4,2,2,2,1024]{5,4,3,2,1,0:T(2,128)S(1)} %broadcast_multiply_fusion), channel_id=1, source_target_pairs={{0,4},{4,0},{8,12},{12,8},{16,20},{20,16},{24,28},{28,24},{1,5},{5... | collective-permute-start | bytes 3145736 | tf_op jit(solution)/shard_map/ppermute | solution.py:15
  466.6 24.2 %collective-permute-start.7 = (f32[8,4,2,2,2,1024]{5,4,3,2,1,0:T(2,128)S(1)}, f32[8,4,2,2,2,1024]{5,4,3,2,1,0:T(2,128)S(1)}, u32[]{:S(2)}, u32[]{:S(2)}) collective-permute-start(f32[8,4,2,2,2,1024]{5,4,3,2,1,0:T(2,128)S(1)} %fusion.82), channel_id=1, source_target_pairs={{0,8},{4,12},{8,0},{12,4},{16,24},{20,28},{24,16},{28,20},{1,9},{5... | collective-permute-start | bytes 3145736 | tf_op jit(solution)/shard_map/ppermute | solution.py:15
  491.9 47.8 %collective-permute-start.8 = (f32[8,4,2,2,2,1024]{5,4,3,2,1,0:T(2,128)S(1)}, f32[8,4,2,2,2,1024]{5,4,3,2,1,0:T(2,128)S(1)}, u32[]{:S(2)}, u32[]{:S(2)}) collective-permute-start(f32[8,4,2,2,2,1024]{5,4,3,2,1,0:T(2,128)S(1)} %fusion.110), channel_id=1, source_target_pairs={{0,16},{4,20},{8,24},{12,28},{16,0},{20,4},{24,8},{28,12},{1,17},{... | collective-permute-start | bytes 3145736 | tf_op jit(solution)/shard_map/ppermute | solution.py:15
  542.5 4.7 copy-start.1
  (115 other events, 298.2 us)
Sparse Core Ops, SparseCore 0:
  50.2 35.0 all-reduce.4
  161.1 29.5 all-reduce.6
  328.3 33.6 all-reduce.8
